TPU v7x, 256 devices: a whole 4x4x8 slice. The times are simulated.
256 devices in a mesh: seq: 64 (over x_hi, z, y), mp: 4 (over x_lo, core).
Axes of the slice: x: 4 (x_hi: 2, x_lo: 2; x = x_hi * 2 + x_lo), y: 4, z: 8, core: 2. Of those that a mesh axis runs over, the one named last changes fastest.
Arguments:
- gate_in: bfloat16 [65536, 1024], P('seq', 'mp'), may hold values from -5 to 5
- value_in: bfloat16 [65536, 1024], P('seq', 'mp'), may hold values from -5 to 5
- out_gate: bfloat16 [65536, 1024], P('seq', 'mp'), may hold values from -10 to 10
- filter_taps: bfloat16 [4096, 1024], P('seq', 'mp'), may hold values from -0.09375 to 0.09375
- skip_gain: float32 [1024], P('mp'), may hold values from -4 to 4
Outputs:
- output: bfloat16 [65536, 1024], P('seq', 'mp')
All inputs are finite; a program needn't handle non-finite values.
Results may differ from a plain program's by a relative error of at most 0.009.
Values may be sent and summed in bfloat16 or wider, within the bound.
A program may use at most 64 MiB of HBM per device.

v0:
```python
import math

import jax
import jax.numpy as jnp
from jax import lax
from jax.sharding import PartitionSpec as P

C = 1024
K = 4096
P_SIZE = 128


def shortened(shard):
    return jax.tree.map(lambda a: a.astype(jnp.bfloat16) if a.dtype == jnp.float32 else a, shard)


def from_everyone(shard, axis):
    copies = jnp.broadcast_to(shard, (lax.axis_size(axis), *shard.shape))
    return lax.all_to_all(copies, axis, split_axis=0, concat_axis=0, tiled=True)


def over_copies(shard, axis):
    everything = from_everyone(shard, axis)
    return jnp.sum(everything, axis=0)


def dft_tables(block):
    frame_len = 2 * block
    sample = lax.iota(jnp.int32, frame_len)[:, None]
    frequency = lax.iota(jnp.int32, block)[None, :]
    angles = (sample * frequency % frame_len).astype(jnp.float32) * (2.0 * math.pi / frame_len)
    alternate = jnp.where(sample % 2 == 0, 1.0, -1.0).astype(jnp.float32)
    forward = jnp.concatenate(
        [jnp.cos(angles), jnp.where(frequency == 0, alternate, -jnp.sin(angles))], axis=1
    )
    later = block + lax.iota(jnp.int32, block)[None, :]
    column = lax.iota(jnp.int32, block)[:, None]
    back_angles = (column * later % frame_len).astype(jnp.float32) * (2.0 * math.pi / frame_len)
    back_sign = jnp.where(later % 2 == 0, 1.0, -1.0).astype(jnp.float32)
    inv_real = jnp.where(column == 0, 1.0, 2.0 * jnp.cos(back_angles)) / frame_len
    inv_imag = jnp.where(column == 0, back_sign, -2.0 * jnp.sin(back_angles)) / frame_len
    backward = jnp.concatenate([inv_real, inv_imag], axis=0)
    return (forward, backward)


def split_table(table):
    upper_part = table.astype(jnp.bfloat16)
    lower_part = (table - upper_part.astype(jnp.float32)).astype(jnp.bfloat16)
    return (upper_part, lower_part)


def transform_rows(form, data, table):
    upper_part, lower_part = split_table(table)
    first = jnp.einsum(form, data, upper_part, preferred_element_type=jnp.float32)
    return first + jnp.einsum(form, data, lower_part, preferred_element_type=jnp.float32)


def filter_spectra(portion):
    forward, backward = dft_tables(P_SIZE)
    channels = portion.shape[1]
    segments = portion.reshape(-1, P_SIZE, channels)
    return transform_rows("snc,nf->scf", segments, forward[:P_SIZE])


def convolve(window, filter_spec):
    forward, backward = dft_tables(P_SIZE)
    channels = window.shape[1]
    blocks = window.reshape(-1, P_SIZE, channels)
    frames = jnp.concatenate([blocks[:-1], blocks[1:]], axis=1)
    spectra = transform_rows("mnc,nf->mcf", frames, forward)
    frame_count = spectra.shape[0]
    seg_count = filter_spec.shape[0]
    features = channels * 2 * P_SIZE
    lhs_data = spectra.reshape(1, frame_count, features)
    spec_real = filter_spec[..., :P_SIZE]
    spec_imag = filter_spec[..., P_SIZE:]
    kernel_real = jnp.concatenate([spec_real, spec_real], axis=-1)
    kernel_imag = jnp.concatenate([spec_imag, spec_imag], axis=-1)
    kernel = jnp.stack([kernel_real, kernel_imag], axis=-1)[::-1].reshape(
        seg_count, 1, features * 2
    )
    merged = lax.conv_general_dilated(
        lhs_data,
        kernel,
        (1,),
        "VALID",
        dimension_numbers=("NWC", "WIO", "NWC"),
        feature_group_count=features,
        precision=lax.Precision.HIGH,
    )
    merged = merged.reshape(-1, channels, 2 * P_SIZE, 2)
    with_real = merged[..., 0]
    with_imag = merged[..., 1]
    first_col = lax.iota(jnp.int32, P_SIZE) == 0
    out_real = with_real[..., :P_SIZE] - jnp.where(first_col, 0.0, with_imag[..., P_SIZE:])
    out_imag = jnp.where(
        first_col, with_imag[..., P_SIZE:], with_imag[..., :P_SIZE] + with_real[..., P_SIZE:]
    )
    joined = jnp.concatenate([out_real, out_imag], axis=-1)
    result = jnp.einsum("bcf,fn->bnc", joined, backward, precision=lax.Precision.HIGH)
    return result.reshape(-1, channels)


def local(gate_in, value_in, out_gate, filter_taps, skip_gain):
    gated = (gate_in.astype(jnp.float32) * value_in.astype(jnp.float32)).astype(jnp.bfloat16)
    by_channel, taps_channel = (
        lax.all_to_all(gated, "seq", split_axis=1, concat_axis=0, tiled=True),
        lax.all_to_all(filter_taps, "seq", split_axis=1, concat_axis=0, tiled=True),
    )
    leading = jnp.zeros((K, by_channel.shape[1]), jnp.bfloat16)
    window = jnp.concatenate([leading, by_channel], axis=0)
    filter_spec = filter_spectra(taps_channel)
    channel_result = convolve(window, filter_spec)
    convolved = lax.all_to_all(
        shortened(channel_result), "seq", split_axis=0, concat_axis=1, tiled=True
    ).astype(channel_result.dtype)
    gated_out = out_gate.astype(jnp.float32) * (
        convolved + skip_gain[None, :] * gated.astype(jnp.float32)
    )
    squares = jnp.sum(gated_out * gated_out, axis=1)
    totals = over_copies(squares, "mp")
    return (gated_out / jnp.sqrt(totals[:, None] / C + 1e-05)).astype(jnp.bfloat16)


def solution(mesh):
    return jax.shard_map(
        local,
        mesh=mesh,
        in_specs=(P("seq", "mp"), P("seq", "mp"), P("seq", "mp"), P("seq", "mp"), P("mp")),
        out_specs=P("seq", "mp"),
        check_vma=False,
    )
```

profile of v0, /device:TPU:1, one launch (start us, length us, event | category | flops | bytes accessed | tf_op | source)
XLA Modules:
  0.0 138.5 jit_solution(6606847997319983063)
XLA Ops:
  0.0 0.9 copy.56
  0.9 0.7 reshape.118
  1.6 15.1 %all-to-all-start.1 = ((bf16[64,2,128]{2,1,0:T(2,128)(2,1)}), bf16[64,2,128]{2,1,0:T(2,128)(2,1)S(1)}, u32[]{:S(2)}, u32[]{:S(2)}) async-start(bf16[64,2,128]{2,1,0:T(2,128)(2,1)} %reshape.118), calls=%async_computation.1 | async-start | bytes 65536 | tf_op jit(solution)/shard_map/all_to_all | solution.py:108
  16.7 1.2 copy.53
  18.0 1.2 copy.54
  19.2 0.5 negate_select_fusion.2
  20.3 1.0 all_to_all.38
  21.3 6.3 %all-to-all-done.1 = bf16[64,2,128]{2,1,0:T(2,128)(2,1)S(1)} async-done(((bf16[64,2,128]{2,1,0:T(2,128)(2,1)}), bf16[64,2,128]{2,1,0:T(2,128)(2,1)S(1)}, u32[]{:S(2)}, u32[]{:S(2)}) %all-to-all-start.1) | async-done | bytes 32800 | tf_op jit(solution)/shard_map/all_to_all | solution.py:108
  27.6 6.1 %all-to-all-start = ((bf16[1024,64,4]{0,2,1:T(4,128)(2,1)}), bf16[1024,64,4]{0,2,1:T(4,128)(2,1)S(1)}, u32[]{:S(2)}, u32[]{:S(2)}) async-start(bf16[1024,64,4]{0,2,1:T(4,128)(2,1)} %all_to_all.38), calls=%async_computation | async-start | bytes 1048576 | tf_op jit(solution)/shard_map/all_to_all | solution.py:107
  35.0 15.3 %all-to-all-done = bf16[1024,64,4]{0,2,1:T(4,128)(2,1)S(1)} async-done(((bf16[1024,64,4]{0,2,1:T(4,128)(2,1)}), bf16[1024,64,4]{0,2,1:T(4,128)(2,1)S(1)}, u32[]{:S(2)}, u32[]{:S(2)}) %all-to-all-start) | async-done | bytes 524320 | tf_op jit(solution)/shard_map/all_to_all | solution.py:107
  50.7 0.8 slice.41
  51.6 0.8 slice.43
  52.6 0.5 fusion.14
  53.5 1.4 %copy.55 = f32[543,4,256]{2,1,0:T(4,128)S(1)} copy(f32[543,4,256]{2,0,1:T(8,128)S(1)} %convolution_add_fusion) | data formatting | bytes 4448256 | tf_op jit(solution)/shard_map/add | solution.py:55
  54.9 4.0 %reshape.115 = f32[1,543,1024,1]{2,0,3,1:T(1,128)} reshape(f32[543,4,256]{2,1,0:T(4,128)S(1)} %copy.55) | data formatting | bytes 4448256 | tf_op jit(solution)/shard_map/reshape.1
  59.0 30.5 %convolution_reduce_fusion = f32[512,1024,2]{1,2,0:T(2,128)} fusion(f32[1,543,1024,1]{2,0,3,1:T(1,128)} %reshape.115, f32[32,1,1024,2]{2,1,3,0:T(1,128)S(1)} %reshape.116), kind=kOutput, calls=%fused_computation.19 | convolution fusion | flops 201326592 | bytes 6680576 | tf_op jit(solution)/shard_map/convolution
  89.5 7.0 %reshape.108 = f32[512,4,256,2]{2,1,3,0:T(4,128)} reshape(f32[512,1024,2]{1,2,0:T(2,128)} %convolution_reduce_fusion) | data formatting | bytes 8388608 | tf_op jit(solution)/shard_map/reshape | solution.py:91
  96.4 2.9 %fusion.48 = (f32[512,4,256,1]{2,1,3,0:T(4,128)S(1)}, f32[512,4,256,1]{2,1,3,0:T(4,128)S(1)}) fusion(f32[512,4,256,2]{2,1,3,0:T(4,128)} %reshape.108), kind=kLoop, calls=%fused_computation.82 | loop fusion | bytes 8388608 | tf_op jit(solution)/shard_map/slice | solution.py:93
  100.4 1.2 fusion.7
  102.2 1.2 copy.64
  103.4 7.3 %all-to-all-start.2 = ((bf16[64,1024,4]{1,2,0:T(4,128)(2,1)}), bf16[64,1024,4]{1,2,0:T(4,128)(2,1)S(1)}, u32[]{:S(2)}, u32[]{:S(2)}) async-start(bf16[64,1024,4]{1,2,0:T(4,128)(2,1)} %copy.64), calls=%async_computation.2 | async-start | bytes 1048576 | tf_op jit(solution)/shard_map/all_to_all | solution.py:114
  110.9 16.0 %all-to-all-done.2 = bf16[64,1024,4]{1,2,0:T(4,128)(2,1)S(1)} async-done(((bf16[64,1024,4]{1,2,0:T(4,128)(2,1)}), bf16[64,1024,4]{1,2,0:T(4,128)(2,1)S(1)}, u32[]{:S(2)}, u32[]{:S(2)}) %all-to-all-start.2) | async-done | bytes 524320 | tf_op jit(solution)/shard_map/all_to_all | solution.py:114
  127.7 9.5 %all_to_all.51 = f32[4,1,1024]{2,1,0:T(1,128)S(1)} all-to-all(f32[4,1,1024]{2,1,0:T(1,128)S(1)} %broadcast_in_dim.103), channel_id=1, replica_groups=mesh['seq'=64,'mp'=4] {'mp'}, dimensions={0} | all-to-all | bytes 32768 | tf_op jit(solution)/shard_map/all_to_all | solution.py:19
  137.5 1.0 copy.66
  (40 shorter events, 5.6 us)
Async XLA Ops:
  1.6 26.0 %all-to-all-start.1 = ((bf16[64,2,128]{2,1,0:T(2,128)(2,1)}), bf16[64,2,128]{2,1,0:T(2,128)(2,1)S(1)}, u32[]{:S(2)}, u32[]{:S(2)}) async-start(bf16[64,2,128]{2,1,0:T(2,128)(2,1)} %reshape.118), calls=%async_computation.1 | async-start | bytes 65536 | tf_op jit(solution)/shard_map/all_to_all | solution.py:108
  27.6 22.7 %all-to-all-start = ((bf16[1024,64,4]{0,2,1:T(4,128)(2,1)}), bf16[1024,64,4]{0,2,1:T(4,128)(2,1)S(1)}, u32[]{:S(2)}, u32[]{:S(2)}) async-start(bf16[1024,64,4]{0,2,1:T(4,128)(2,1)} %all_to_all.38), calls=%async_computation | async-start | bytes 1048576 | tf_op jit(solution)/shard_map/all_to_all | solution.py:107
  101.6 9.0 %copy-start = (bf16[1024,256]{1,0:T(8,128)(2,1)S(1)}, bf16[1024,256]{1,0:T(8,128)(2,1)}, u32[]{:S(2)}) copy-start(bf16[1024,256]{1,0:T(8,128)(2,1)} %param.7) | copy-start | bytes 1572868
  103.4 23.5 %all-to-all-start.2 = ((bf16[64,1024,4]{1,2,0:T(4,128)(2,1)}), bf16[64,1024,4]{1,2,0:T(4,128)(2,1)S(1)}, u32[]{:S(2)}, u32[]{:S(2)}) async-start(bf16[64,1024,4]{1,2,0:T(4,128)(2,1)} %copy.64), calls=%async_computation.2 | async-start | bytes 1048576 | tf_op jit(solution)/shard_map/all_to_all | solution.py:114
  110.9 16.5 %copy-start.1 = (f32[256]{0:T(256)S(1)}, f32[256]{0:T(256)}, u32[]{:S(2)}) copy-start(f32[256]{0:T(256)} %param.9) | copy-start | bytes 3076
where the time goes:
time: 140 us; the launch traced here: 139 us
  waiting for transfers between devices  37.6 us (27%)
  matrix products  32.9 us (24%)
  starting transfers between devices  28.5 us (20%)
  local copies, waits for them, and re-layouts  27.6 us (20%)
  blocking collectives  9.49 us (7%)
  other arithmetic  2.11 us (2%)
    another operation x1, matrix products  30.5 us
    all_to_all x1, waiting for transfers between devices, local(): lax.all_to_all(shortened(channel_result), 'seq', split_axis=0, concat_axi...  16 us
    all_to_all x1, waiting for transfers between devices, local(): lax.all_to_all(gated, 'seq', split_axis=1, concat_axis=0, tiled=True)  15.3 us
    all_to_all x1, starting transfers between devices, local(): lax.all_to_all(filter_taps, 'seq', split_axis=1, concat_axis=0, tiled=True)  15.1 us
    all_to_all x1, blocking collectives, from_everyone(): return lax.all_to_all(copies, axis, split_axis=0, concat_axis=0, tiled=True)  9.49 us
    all_to_all x1, starting transfers between devices, local(): lax.all_to_all(shortened(channel_result), 'seq', split_axis=0, concat_axi...  7.28 us
    reshape x1, local copies, waits for them, and re-layouts, convolve(): merged = merged.reshape(-1, channels, 2 * P_SIZE, 2)  6.99 us
    all_to_all x1, waiting for transfers between devices, local(): lax.all_to_all(filter_taps, 'seq', split_axis=1, concat_axis=0, tiled=True)  6.29 us
  transfers between devices with their start and end apart: 3, of which 3 were waited for; matrix products, arithmetic and copies ran while one was open for 4% of the time, Pallas kernels for 0%

commit v1 on v0

v1 whole, which is shorter than its diff:
```python
import jax
import jax.numpy as jnp
from jax import lax
from jax.experimental import pallas as pl
from jax.experimental.pallas import tpu as pltpu
from jax.sharding import PartitionSpec as P

MESH = pl.DeviceIdType.MESH
F32 = jnp.float32
BF16 = jnp.bfloat16

C = 1024
B = 256
N = 64
T = 1024
CH = 256
OWN = CH // N
TAPS = 64
WIN = 128
NWIN = 4096 // WIN
BANDS = 2 * 17 + 1
SIZE = T + 64


def peer(me, o):
    hi = (me // 32 + o // 32) % 2
    z = (me // 4 % 8 + o // 4 % 8) % 8
    y = (me % 4 + o % 4) % 4
    return hi * 32 + z * 4 + y


def put(ref, size, first, count, stride, value):
    for h in range(2):
        ref[pl.ds(h * size + first, count, stride=stride), :] = value[:, 128 * h : 128 * h + 128]


def take(ref, size, first, count, stride=1):
    halves = [ref[pl.ds(h * size + first, count, stride=stride), :] for h in range(2)]
    return jnp.concatenate(halves, axis=1)


def kernel(
    gate, value, out_gate, taps, skip, out,
    send_x, send_t, recv_x, recv_t, stage, og_t, skip_t, win, planes, bands, send_y, recv_y,
    part, recv_p, sx, rx, st, rt, sy, ry, sp, rp,
):
    me = lax.axis_index("seq")
    mp = lax.axis_index("mp")
    barrier = pltpu.get_barrier_semaphore()

    def greet(o, carry):
        pl.semaphore_signal(barrier, inc=1, device_id={"seq": peer(me, o)}, device_id_type=MESH)
        return carry

    lax.fori_loop(1, N, greet, 0)
    for k in range(1, 4):
        pl.semaphore_signal(barrier, inc=1, device_id={"mp": (mp + k) % 4}, device_id_type=MESH)

    wide = jnp.concatenate([taps[...].astype(F32), jnp.zeros((128 - TAPS, CH), F32)], axis=0)
    stage[0:CH, :] = wide.T
    rows = [stage[pl.ds(c, N, stride=OWN), :] for c in range(OWN)]
    pairs = jnp.concatenate(
        [rows[0] + pltpu.roll(rows[1], 64, 1), rows[2] + pltpu.roll(rows[3], 64, 1)], axis=1
    )
    for j in range(N):
        send_t[j] = pairs[j : j + 1]

    for q in range(4):
        at = pl.ds(q * B, B)
        gated = (gate[at, :].astype(F32) * value[at, :].astype(F32)).astype(BF16)
        put(stage, SIZE, q, CH, 4, gated.astype(F32).T)
    for j in range(0, N, 8):
        send_x[pl.ds(j, 8)] = take(stage, SIZE, j * 16, 128).astype(BF16).reshape(8, 16, B)
    for q in range(4):
        put(og_t, T, q, CH, 4, out_gate[pl.ds(q * B, B), :].astype(F32).T)
        skip_t[pl.ds(q, CH, stride=4), :] = jnp.broadcast_to(skip[...], (128, CH)).T

    pl.semaphore_wait(barrier, N - 1 + 3)

    def send(src, dst, ssem, rsem):
        def one(o, carry):
            to = peer(me, o)
            pltpu.make_async_remote_copy(
                src.at[to], dst.at[me], ssem, rsem, device_id={"seq": to}, device_id_type=MESH
            ).start()
            return carry

        lax.fori_loop(1, N, one, 0)

    def waits(src, dst, ssem, rsem):
        return pltpu.make_async_remote_copy(
            src.at[pl.ds(0, N - 1)], dst.at[pl.ds(0, N - 1)], ssem, rsem,
            device_id={"seq": peer(me, 1)}, device_id_type=MESH,
        )

    send(send_t, recv_t, st, rt)
    send(send_x, recv_x, sx, rx)
    recv_t[me] = send_t[me]
    recv_x[me] = send_x[me]

    waits(send_t, recv_t, st, rt).wait_recv()
    lane = lax.broadcasted_iota(jnp.int32, (1, WIN), 1)
    win[...] = jnp.zeros_like(win)
    for j in range(NWIN):
        even, odd = recv_t[2 * j], recv_t[2 * j + 1]
        for c in range(OWN):
            half = slice(c // 2 * 128, c // 2 * 128 + 128)
            e, d = even[:, half], odd[:, half]
            row = jnp.where(lane < 64, e, pltpu.roll(d, 64, 1)) if c % 2 == 0 else (
                jnp.where(lane < 64, pltpu.roll(e, 64, 1), d)
            )
            win[c, pl.ds(j + 1, 1), :] = row
    after = lax.broadcasted_iota(jnp.int32, (WIN, WIN), 1) >= lax.broadcasted_iota(
        jnp.int32, (WIN, WIN), 0
    )
    for c in range(OWN):
        bands[c, pl.ds(0, WIN), :] = jnp.zeros((WIN, WIN), BF16)
        bands[c, pl.ds((BANDS - 1) * WIN, WIN), :] = jnp.zeros((WIN, WIN), BF16)

        def band(v, before, c=c):
            row = jnp.broadcast_to(win[c, pl.ds(v + 1, 1), :], (WIN, WIN))
            rolled = pltpu.roll(row, 0, 1, stride=1, stride_axis=0)
            at = pl.multiple_of((BANDS - 2 - v) * WIN, WIN)
            bands[c, pl.ds(at, WIN), :] = jnp.where(after, rolled, before).astype(BF16)
            return rolled

        lax.fori_loop(0, NWIN + 1, band, jnp.zeros((WIN, WIN), F32))

    waits(send_x, recv_x, sx, rx).wait_recv()
    put(stage, SIZE, 0, 64, 1, jnp.zeros((64, B), F32))
    for j in range(0, N, 8):
        put(stage, SIZE, 64 + j * 16, 128, 1, recv_x[pl.ds(j, 8)].reshape(128, B).astype(F32))
    for c in range(OWN):
        for a in range(16):
            first = 16 * (a // 4) + 4 * c + a % 4
            for late in range(2):
                rows = take(stage, SIZE, first + 64 * late, 16, 64)
                planes[c, pl.ds(256 * late + 16 * a, 16), :] = rows.astype(BF16)

    for c in range(OWN):
        total = jnp.zeros((256, B), F32)
        for d in range(17):
            left = planes[c, pl.ds((16 - d) * 16, 256), :]
            low = bands[c, pl.ds((33 - 2 * d) * WIN, 2 * WIN), :]
            high = bands[c, pl.ds((32 - 2 * d) * WIN, 2 * WIN), :]
            total += jnp.dot(
                left, jnp.concatenate([low, high], axis=1), preferred_element_type=F32
            )
        for a in range(16):
            first = 16 * (a // 4) + 4 * c + a % 4
            put(stage, SIZE, first, 16, 64, total[16 * a : 16 * a + 16])
    for j in range(0, N, 8):
        send_y[pl.ds(j, 8)] = take(stage, SIZE, j * 16, 128).astype(BF16).reshape(8, 16, B)
    recv_y[me] = send_y[me]
    send(send_y, recv_y, sy, ry)
    waits(send_y, recv_y, sy, ry).wait_recv()

    squares = jnp.zeros((8, B), F32)
    for j in range(0, N, 2):
        at = pl.ds(j * 16, 32)
        gain = skip_t[at, :]
        conv = recv_y[pl.ds(j, 2)].reshape(32, B).astype(F32)
        gated = send_x[pl.ds(j, 2)].reshape(32, B).astype(F32)
        mixed = take(og_t, T, j * 16, 32) * (conv + jnp.concatenate([gain, gain], axis=1) * gated)
        put(stage, SIZE, j * 16, 32, 1, mixed)
        squares += jnp.sum((mixed * mixed).reshape(4, 8, B), axis=0)
    part[0:4, :] = squares[0:4] + squares[4:8]
    part[4:8, :] = jnp.zeros((4, B), F32)
    copies = []
    for k in range(1, 4):
        copy = pltpu.make_async_remote_copy(
            part, recv_p.at[k - 1], sp.at[k - 1], rp.at[k - 1],
            device_id={"mp": (mp + k) % 4}, device_id_type=MESH,
        )
        copy.start()
        copies.append(copy)
    power = part[0:4, :]
    for copy in copies:
        copy.wait_recv()
    power = power + recv_p[0][0:4] + recv_p[1][0:4] + recv_p[2][0:4]
    scale = 1.0 / jnp.sqrt(power / C + 1e-05)
    for q in range(4):
        mixed = take(stage, SIZE, q, CH, 4) * scale[q : q + 1]
        out[pl.ds(q * B, B), :] = mixed.T.astype(BF16)
    for copy in copies:
        copy.wait_send()
    waits(send_t, recv_t, st, rt).wait_send()
    waits(send_x, recv_x, sx, rx).wait_send()
    waits(send_y, recv_y, sy, ry).wait_send()


def local(gate_in, value_in, out_gate, filter_taps, skip_gain):
    vmem = pl.BlockSpec(memory_space=pltpu.VMEM)
    dma = pltpu.SemaphoreType.DMA
    return pl.pallas_call(
        kernel,
        out_shape=jax.ShapeDtypeStruct((T, CH), BF16),
        in_specs=[vmem] * 5,
        out_specs=vmem,
        scratch_shapes=[
            pltpu.VMEM((N, 16, B), BF16),
            pltpu.VMEM((N, 1, B), F32),
            pltpu.VMEM((N, 16, B), BF16),
            pltpu.VMEM((N, 1, B), F32),
            pltpu.VMEM((2 * SIZE, 128), F32),
            pltpu.VMEM((2 * T, 128), F32),
            pltpu.VMEM((T, 128), F32),
            pltpu.VMEM((OWN, 40, WIN), F32),
            pltpu.VMEM((OWN, 512, B), BF16),
            pltpu.VMEM((OWN, BANDS * WIN, WIN), BF16),
            pltpu.VMEM((N, 16, B), BF16),
            pltpu.VMEM((N, 16, B), BF16),
            pltpu.VMEM((8, B), F32),
            pltpu.VMEM((3, 8, B), F32),
            dma, dma, dma, dma, dma, dma, dma((3,)), dma((3,)),
        ],
        compiler_params=pltpu.CompilerParams(
            collective_id=0, has_side_effects=True, vmem_limit_bytes=48 * 2**20
        ),
    )(gate_in, value_in, out_gate, filter_taps, skip_gain.reshape(1, CH))


def solution(mesh):
    return jax.shard_map(
        local,
        mesh=mesh,
        in_specs=(P("seq", "mp"), P("seq", "mp"), P("seq", "mp"), P("seq", "mp"), P("mp")),
        out_specs=P("seq", "mp"),
        check_vma=False,
    )
```

time: 140 us -> 62.1 us (0.44)
  Pallas kernels: 0 us -> 56.5 us
  waiting for transfers between devices: 37.6 us -> 0 us
  matrix products: 32.9 us -> 0 us
  starting transfers between devices: 28.5 us -> 0 us
  local copies, waits for them, and re-layouts: 27.6 us -> 5.35 us
  blocking collectives: 9.49 us -> 0 us
  other arithmetic: 2.11 us -> 0 us
    pallas_call x0 -> x1, Pallas kernels: none -> 56.5 us  [local(): pl.pallas_call(kernel, out_shape=jax.ShapeDtypeStruct((T, CH), BF16), in_...]
    all_to_all x3 -> x0, waiting for transfers between devices: 37.6 us -> none  [the longest x1 16 us: local(): lax.all_to_all(shortened(channel_result), 'seq', split_axis=0, concat_axi...]
    another operation x1 -> x0, matrix products: 30.5 us -> none
    all_to_all x3 -> x0, starting transfers between devices: 28.5 us -> none  [the longest x1 15.1 us: local(): lax.all_to_all(filter_taps, 'seq', split_axis=1, concat_axis=0, tiled=True)]
    all_to_all x1 -> x0, blocking collectives: 9.49 us -> none  [from_everyone(): return lax.all_to_all(copies, axis, split_axis=0, concat_axis=0, tiled=True)]
    reshape x4 -> x0, local copies, waits for them, and re-layouts: 7.58 us -> none  [the longest x1 6.99 us: convolve(): merged = merged.reshape(-1, channels, 2 * P_SIZE, 2)]
    slice x5 -> x0, local copies, waits for them, and re-layouts: 4.95 us -> none  [the longest x1 2.94 us: convolve(): with_imag = merged[..., 1]]
    another operation x1 -> x0, local copies, waits for them, and re-layouts: 4.04 us -> none
  transfers between devices with their start and end apart: 3 -> 0, of which waited for: 3 -> 0; matrix products, arithmetic and copies ran while one was open for 4% -> 0% of each run, Pallas kernels for 0% -> 0%
where the time goes in v1:
time: 62.1 us; the launch traced here: 61.8 us
  Pallas kernels  56.5 us (91%)
  local copies, waits for them, and re-layouts  5.35 us (9%)
    pallas_call x1, Pallas kernels, local(): pl.pallas_call(kernel, out_shape=jax.ShapeDtypeStruct((T, CH), BF16), in_...  56.5 us
    unnamed x11, local copies, waits for them, and re-layouts  5.35 us

profile of v1, /device:TPU:1, one launch (start us, length us, event | category | flops | bytes accessed | tf_op | source)
XLA Modules:
  0.0 61.8 jit_solution(15112305382997648714)
XLA Ops:
  0.0 0.0 copy-start.4
  0.0 0.7 %copy-done.4 = f32[256]{0:T(256)S(1)} copy-done((f32[256]{0:T(256)S(1)}, f32[256]{0:T(256)}, u32[]{:S(2)}) %copy-start.4) | copy-done | bytes 1048
  0.7 0.0 copy-start
  0.7 1.0 %copy-done = bf16[1024,256]{1,0:T(8,128)(2,1)S(1)} copy-done((bf16[1024,256]{1,0:T(8,128)(2,1)S(1)}, bf16[1024,256]{1,0:T(8,128)(2,1)}, u32[]{:S(2)}) %copy-start) | copy-done | bytes 524312
  1.7 0.0 copy-start.1
  1.7 1.0 %copy-done.1 = bf16[1024,256]{1,0:T(8,128)(2,1)S(1)} copy-done((bf16[1024,256]{1,0:T(8,128)(2,1)S(1)}, bf16[1024,256]{1,0:T(8,128)(2,1)}, u32[]{:S(2)}) %copy-start.1) | copy-done | bytes 524312
  2.8 0.0 copy-start.2
  2.8 1.0 %copy-done.2 = bf16[1024,256]{1,0:T(8,128)(2,1)S(1)} copy-done((bf16[1024,256]{1,0:T(8,128)(2,1)S(1)}, bf16[1024,256]{1,0:T(8,128)(2,1)}, u32[]{:S(2)}) %copy-start.2) | copy-done | bytes 524312
  3.8 0.0 copy-start.3
  3.8 0.8 %copy-done.3 = bf16[64,256]{1,0:T(8,128)(2,1)S(1)} copy-done((bf16[64,256]{1,0:T(8,128)(2,1)S(1)}, bf16[64,256]{1,0:T(8,128)(2,1)}, u32[]{:S(2)}) %copy-start.3) | copy-done | bytes 32792
  4.6 56.5 %shard_map.55 = bf16[1024,256]{1,0:T(8,128)(2,1)S(1)} custom-call(bf16[1024,256]{1,0:T(8,128)(2,1)S(1)} %copy-done, bf16[1024,256]{1,0:T(8,128)(2,1)S(1)} %copy-done.1, bf16[1024,256]{1,0:T(8,128)(2,1)S(1)} %copy-done.2, bf16[64,256]{1,0:T(8,128)(2,1)S(1)} %copy-done.3, f32[1,256]{1,0:T(1,128)S(1)} %bitcast.1), custom_call_target="tpu_custom_call" | custom-call | tf_op jit(solution)/shard_map/pallas_call | solution.py:195
  61.0 0.8 %copy.7 = bf16[1024,256]{1,0:T(8,128)(2,1)} copy(bf16[1024,256]{1,0:T(8,128)(2,1)S(1)} %shard_map.55) | data formatting | bytes 1048576
Async XLA Ops:
  0.0 0.7 %copy-start.4 = (f32[256]{0:T(256)S(1)}, f32[256]{0:T(256)}, u32[]{:S(2)}) copy-start(f32[256]{0:T(256)} %param.9) | copy-start | bytes 3076
  0.7 1.0 %copy-start = (bf16[1024,256]{1,0:T(8,128)(2,1)S(1)}, bf16[1024,256]{1,0:T(8,128)(2,1)}, u32[]{:S(2)}) copy-start(bf16[1024,256]{1,0:T(8,128)(2,1)} %gate.1) | copy-start | bytes 1572868
  1.7 1.0 %copy-start.1 = (bf16[1024,256]{1,0:T(8,128)(2,1)S(1)}, bf16[1024,256]{1,0:T(8,128)(2,1)}, u32[]{:S(2)}) copy-start(bf16[1024,256]{1,0:T(8,128)(2,1)} %value.1) | copy-start | bytes 1572868
  2.8 1.0 %copy-start.2 = (bf16[1024,256]{1,0:T(8,128)(2,1)S(1)}, bf16[1024,256]{1,0:T(8,128)(2,1)}, u32[]{:S(2)}) copy-start(bf16[1024,256]{1,0:T(8,128)(2,1)} %out_gate.1) | copy-start | bytes 1572868
  3.8 0.8 %copy-start.3 = (bf16[64,256]{1,0:T(8,128)(2,1)S(1)}, bf16[64,256]{1,0:T(8,128)(2,1)}, u32[]{:S(2)}) copy-start(bf16[64,256]{1,0:T(8,128)(2,1)} %taps.1) | copy-start | bytes 98308

commit v2 on v1

--- a/solution.py
+++ b/solution.py
@@ -40,9 +40,10 @@
 
 
 def kernel(
-    gate, value, out_gate, taps, skip, out,
+    gate_h, value_h, out_gate_h, taps_h, skip_h, out,
+    gate, value, out_gate, taps, skip,
     send_x, send_t, recv_x, recv_t, stage, og_t, skip_t, win, planes, bands, send_y, recv_y,
-    part, recv_p, sx, rx, st, rt, sy, ry, sp, rp,
+    part, recv_p, loaded, sx, rx, st, rt, sy, ry, sp, rp,
 ):
     me = lax.axis_index("seq")
     mp = lax.axis_index("mp")
@@ -56,6 +57,12 @@
     for k in range(1, 4):
         pl.semaphore_signal(barrier, inc=1, device_id={"mp": (mp + k) % 4}, device_id_type=MESH)
 
+    pairs = ((taps_h, taps), (gate_h, gate), (value_h, value), (out_gate_h, out_gate), (skip_h, skip))
+    loads = [pltpu.make_async_copy(a, b, loaded.at[i]) for i, (a, b) in enumerate(pairs)]
+    for load in loads:
+        load.start()
+
+    loads[0].wait()
     wide = jnp.concatenate([taps[...].astype(F32), jnp.zeros((128 - TAPS, CH), F32)], axis=0)
     stage[0:CH, :] = wide.T
     rows = [stage[pl.ds(c, N, stride=OWN), :] for c in range(OWN)]
@@ -65,16 +72,14 @@
     for j in range(N):
         send_t[j] = pairs[j : j + 1]
 
+    loads[1].wait()
+    loads[2].wait()
     for q in range(4):
         at = pl.ds(q * B, B)
         gated = (gate[at, :].astype(F32) * value[at, :].astype(F32)).astype(BF16)
         put(stage, SIZE, q, CH, 4, gated.astype(F32).T)
     for j in range(0, N, 8):
         send_x[pl.ds(j, 8)] = take(stage, SIZE, j * 16, 128).astype(BF16).reshape(8, 16, B)
-    for q in range(4):
-        put(og_t, T, q, CH, 4, out_gate[pl.ds(q * B, B), :].astype(F32).T)
-        skip_t[pl.ds(q, CH, stride=4), :] = jnp.broadcast_to(skip[...], (128, CH)).T
-
     pl.semaphore_wait(barrier, N - 1 + 3)
 
     def send(src, dst, ssem, rsem):
@@ -97,6 +102,12 @@
     send(send_x, recv_x, sx, rx)
     recv_t[me] = send_t[me]
     recv_x[me] = send_x[me]
+
+    loads[3].wait()
+    loads[4].wait()
+    for q in range(4):
+        put(og_t, T, q, CH, 4, out_gate[pl.ds(q * B, B), :].astype(F32).T)
+        skip_t[pl.ds(q, CH, stride=4), :] = jnp.broadcast_to(skip[...], (128, CH)).T
 
     waits(send_t, recv_t, st, rt).wait_recv()
     lane = lax.broadcasted_iota(jnp.int32, (1, WIN), 1)
@@ -113,18 +124,19 @@
     after = lax.broadcasted_iota(jnp.int32, (WIN, WIN), 1) >= lax.broadcasted_iota(
         jnp.int32, (WIN, WIN), 0
     )
-    for c in range(OWN):
+    def banded(c, carry):
+        before = jnp.zeros((WIN, WIN), F32)
+        bands[c, pl.ds((BANDS - 1) * WIN, WIN), :] = before.astype(BF16)
+        for v in range(NWIN + 1):
+            row = jnp.broadcast_to(win[c, v + 1 : v + 2, :], (WIN, WIN))
+            rolled = pltpu.roll(row, 0, 1, stride=1, stride_axis=0)
+            at = pl.ds((BANDS - 2 - v) * WIN, WIN)
+            bands[c, at, :] = jnp.where(after, rolled, before).astype(BF16)
+            before = rolled
         bands[c, pl.ds(0, WIN), :] = jnp.zeros((WIN, WIN), BF16)
-        bands[c, pl.ds((BANDS - 1) * WIN, WIN), :] = jnp.zeros((WIN, WIN), BF16)
-
-        def band(v, before, c=c):
-            row = jnp.broadcast_to(win[c, pl.ds(v + 1, 1), :], (WIN, WIN))
-            rolled = pltpu.roll(row, 0, 1, stride=1, stride_axis=0)
-            at = pl.multiple_of((BANDS - 2 - v) * WIN, WIN)
-            bands[c, pl.ds(at, WIN), :] = jnp.where(after, rolled, before).astype(BF16)
-            return rolled
-
-        lax.fori_loop(0, NWIN + 1, band, jnp.zeros((WIN, WIN), F32))
+        return carry
+
+    lax.fori_loop(0, OWN, banded, 0)
 
     waits(send_x, recv_x, sx, rx).wait_recv()
     put(stage, SIZE, 0, 64, 1, jnp.zeros((64, B), F32))
@@ -195,9 +207,14 @@
     return pl.pallas_call(
         kernel,
         out_shape=jax.ShapeDtypeStruct((T, CH), BF16),
-        in_specs=[vmem] * 5,
+        in_specs=[pl.BlockSpec(memory_space=pltpu.HBM)] * 5,
         out_specs=vmem,
         scratch_shapes=[
+            pltpu.VMEM((T, CH), BF16),
+            pltpu.VMEM((T, CH), BF16),
+            pltpu.VMEM((T, CH), BF16),
+            pltpu.VMEM((TAPS, CH), BF16),
+            pltpu.VMEM((1, CH), F32),
             pltpu.VMEM((N, 16, B), BF16),
             pltpu.VMEM((N, 1, B), F32),
             pltpu.VMEM((N, 16, B), BF16),
@@ -212,7 +229,7 @@
             pltpu.VMEM((N, 16, B), BF16),
             pltpu.VMEM((8, B), F32),
             pltpu.VMEM((3, 8, B), F32),
-            dma, dma, dma, dma, dma, dma, dma((3,)), dma((3,)),
+            dma((5,)), dma, dma, dma, dma, dma, dma, dma((3,)), dma((3,)),
         ],
         compiler_params=pltpu.CompilerParams(
             collective_id=0, has_side_effects=True, vmem_limit_bytes=48 * 2**20

time: 62.1 us -> 61 us (0.982)
  Pallas kernels: 56.5 us -> 55.4 us
    pallas_call x1, Pallas kernels: 56.5 us -> 55.4 us  [local(): pl.pallas_call(kernel, out_shape=jax.ShapeDtypeStruct((T, CH), BF16), in_...]
where the time goes in v2:
time: 61 us; the launch traced here: 60.7 us
  Pallas kernels  55.4 us (91%)
  local copies, waits for them, and re-layouts  5.35 us (9%)
    pallas_call x1, Pallas kernels, local(): pl.pallas_call(kernel, out_shape=jax.ShapeDtypeStruct((T, CH), BF16), in_...  55.4 us
    unnamed x11, local copies, waits for them, and re-layouts  5.35 us

profile of v2, /device:TPU:1, one launch (start us, length us, event | category | flops | bytes accessed | tf_op | source)
XLA Modules:
  0.0 60.7 jit_solution(12144336480232383713)
XLA Ops:
  0.0 0.0 copy-start.4
  0.0 0.7 %copy-done.4 = f32[256]{0:T(256)S(1)} copy-done((f32[256]{0:T(256)S(1)}, f32[256]{0:T(256)}, u32[]{:S(2)}) %copy-start.4) | copy-done | bytes 1048
  0.7 0.0 copy-start
  0.7 1.0 %copy-done = bf16[1024,256]{1,0:T(8,128)(2,1)S(1)} copy-done((bf16[1024,256]{1,0:T(8,128)(2,1)S(1)}, bf16[1024,256]{1,0:T(8,128)(2,1)}, u32[]{:S(2)}) %copy-start) | copy-done | bytes 524312
  1.7 0.0 copy-start.1
  1.7 1.0 %copy-done.1 = bf16[1024,256]{1,0:T(8,128)(2,1)S(1)} copy-done((bf16[1024,256]{1,0:T(8,128)(2,1)S(1)}, bf16[1024,256]{1,0:T(8,128)(2,1)}, u32[]{:S(2)}) %copy-start.1) | copy-done | bytes 524312
  2.8 0.0 copy-start.2
  2.8 1.0 %copy-done.2 = bf16[1024,256]{1,0:T(8,128)(2,1)S(1)} copy-done((bf16[1024,256]{1,0:T(8,128)(2,1)S(1)}, bf16[1024,256]{1,0:T(8,128)(2,1)}, u32[]{:S(2)}) %copy-start.2) | copy-done | bytes 524312
  3.8 0.0 copy-start.3
  3.8 0.8 %copy-done.3 = bf16[64,256]{1,0:T(8,128)(2,1)S(1)} copy-done((bf16[64,256]{1,0:T(8,128)(2,1)S(1)}, bf16[64,256]{1,0:T(8,128)(2,1)}, u32[]{:S(2)}) %copy-start.3) | copy-done | bytes 32792
  4.6 55.4 %shard_map.55 = bf16[1024,256]{1,0:T(8,128)(2,1)S(1)} custom-call(bf16[1024,256]{1,0:T(8,128)(2,1)S(1)} %copy-done, bf16[1024,256]{1,0:T(8,128)(2,1)S(1)} %copy-done.1, bf16[1024,256]{1,0:T(8,128)(2,1)S(1)} %copy-done.2, bf16[64,256]{1,0:T(8,128)(2,1)S(1)} %copy-done.3, f32[1,256]{1,0:T(1,128)S(1)} %bitcast.1), custom_call_target="tpu_custom_call" | custom-call | tf_op jit(solution)/shard_map/pallas_call | solution.py:207
  59.9 0.8 %copy.7 = bf16[1024,256]{1,0:T(8,128)(2,1)} copy(bf16[1024,256]{1,0:T(8,128)(2,1)S(1)} %shard_map.55) | data formatting | bytes 1048576
Async XLA Ops:
  0.0 0.7 %copy-start.4 = (f32[256]{0:T(256)S(1)}, f32[256]{0:T(256)}, u32[]{:S(2)}) copy-start(f32[256]{0:T(256)} %param.9) | copy-start | bytes 3076
  0.7 1.0 %copy-start = (bf16[1024,256]{1,0:T(8,128)(2,1)S(1)}, bf16[1024,256]{1,0:T(8,128)(2,1)}, u32[]{:S(2)}) copy-start(bf16[1024,256]{1,0:T(8,128)(2,1)} %gate_h.1) | copy-start | bytes 1572868
  1.7 1.0 %copy-start.1 = (bf16[1024,256]{1,0:T(8,128)(2,1)S(1)}, bf16[1024,256]{1,0:T(8,128)(2,1)}, u32[]{:S(2)}) copy-start(bf16[1024,256]{1,0:T(8,128)(2,1)} %value_h.1) | copy-start | bytes 1572868
  2.8 1.0 %copy-start.2 = (bf16[1024,256]{1,0:T(8,128)(2,1)S(1)}, bf16[1024,256]{1,0:T(8,128)(2,1)}, u32[]{:S(2)}) copy-start(bf16[1024,256]{1,0:T(8,128)(2,1)} %out_gate_h.1) | copy-start | bytes 1572868
  3.8 0.8 %copy-start.3 = (bf16[64,256]{1,0:T(8,128)(2,1)S(1)}, bf16[64,256]{1,0:T(8,128)(2,1)}, u32[]{:S(2)}) copy-start(bf16[64,256]{1,0:T(8,128)(2,1)} %taps_h.1) | copy-start | bytes 98308

commit v3 on v2

--- a/solution.py
+++ b/solution.py
@@ -19,7 +19,10 @@
 WIN = 128
 NWIN = 4096 // WIN
 BANDS = 2 * 17 + 1
-SIZE = T + 64
+GROUPS = 2
+PER = OWN // GROUPS
+ROWS = 4 * PER
+WORK = (N + 4) * ROWS
 
 
 def peer(me, o):
@@ -42,7 +45,7 @@
 def kernel(
     gate_h, value_h, out_gate_h, taps_h, skip_h, out,
     gate, value, out_gate, taps, skip,
-    send_x, send_t, recv_x, recv_t, stage, og_t, skip_t, win, planes, bands, send_y, recv_y,
+    send_x, send_t, recv_x, recv_t, stage, work, turned, og_t, skip_t, win, planes, bands, send_y, recv_y,
     part, recv_p, loaded, sx, rx, st, rt, sy, ry, sp, rp,
 ):
     me = lax.axis_index("seq")
@@ -77,9 +80,11 @@
     for q in range(4):
         at = pl.ds(q * B, B)
         gated = (gate[at, :].astype(F32) * value[at, :].astype(F32)).astype(BF16)
-        put(stage, SIZE, q, CH, 4, gated.astype(F32).T)
+        put(stage, T, q, CH, 4, gated.astype(F32).T)
     for j in range(0, N, 8):
-        send_x[pl.ds(j, 8)] = take(stage, SIZE, j * 16, 128).astype(BF16).reshape(8, 16, B)
+        block = take(stage, T, j * 16, 128).reshape(8, GROUPS, ROWS, B).astype(BF16)
+        for g in range(GROUPS):
+            send_x[g, pl.ds(j, 8)] = block[:, g]
     pl.semaphore_wait(barrier, N - 1 + 3)
 
     def send(src, dst, ssem, rsem):
@@ -99,9 +104,11 @@
         )
 
     send(send_t, recv_t, st, rt)
-    send(send_x, recv_x, sx, rx)
+    for g in range(GROUPS):
+        send(send_x.at[g], recv_x.at[g], sx.at[g], rx.at[g])
     recv_t[me] = send_t[me]
-    recv_x[me] = send_x[me]
+    for g in range(GROUPS):
+        recv_x[g, me] = send_x[g, me]
 
     loads[3].wait()
     loads[4].wait()
@@ -124,6 +131,7 @@
     after = lax.broadcasted_iota(jnp.int32, (WIN, WIN), 1) >= lax.broadcasted_iota(
         jnp.int32, (WIN, WIN), 0
     )
+
     def banded(c, carry):
         before = jnp.zeros((WIN, WIN), F32)
         bands[c, pl.ds((BANDS - 1) * WIN, WIN), :] = before.astype(BF16)
@@ -138,44 +146,48 @@
 
     lax.fori_loop(0, OWN, banded, 0)
 
-    waits(send_x, recv_x, sx, rx).wait_recv()
-    put(stage, SIZE, 0, 64, 1, jnp.zeros((64, B), F32))
-    for j in range(0, N, 8):
-        put(stage, SIZE, 64 + j * 16, 128, 1, recv_x[pl.ds(j, 8)].reshape(128, B).astype(F32))
-    for c in range(OWN):
-        for a in range(16):
-            first = 16 * (a // 4) + 4 * c + a % 4
-            for late in range(2):
-                rows = take(stage, SIZE, first + 64 * late, 16, 64)
-                planes[c, pl.ds(256 * late + 16 * a, 16), :] = rows.astype(BF16)
-
-    for c in range(OWN):
-        total = jnp.zeros((256, B), F32)
-        for d in range(17):
-            left = planes[c, pl.ds((16 - d) * 16, 256), :]
-            low = bands[c, pl.ds((33 - 2 * d) * WIN, 2 * WIN), :]
-            high = bands[c, pl.ds((32 - 2 * d) * WIN, 2 * WIN), :]
-            total += jnp.dot(
-                left, jnp.concatenate([low, high], axis=1), preferred_element_type=F32
+    put(work, WORK, 0, 4 * ROWS, 1, jnp.zeros((4 * ROWS, B), F32))
+    for g in range(GROUPS):
+        waits(send_x.at[g], recv_x.at[g], sx.at[g], rx.at[g]).wait_recv()
+        for j in range(0, N, 8):
+            block = recv_x[g, pl.ds(j, 8)].reshape(8 * ROWS, B).astype(F32)
+            put(work, WORK, (4 + j) * ROWS, 8 * ROWS, 1, block)
+        for c in range(PER):
+            for a in range(16):
+                first = ROWS * (a // 4) + 4 * c + a % 4
+                for late in range(2):
+                    rows = take(work, WORK, first + 4 * ROWS * late, 16, 4 * ROWS)
+                    planes[c, pl.ds(256 * late + 16 * a, 16), :] = rows.astype(BF16)
+        for c in range(PER):
+            total = jnp.zeros((256, B), F32)
+            for d in range(17):
+                left = planes[c, pl.ds((16 - d) * 16, 256), :]
+                low = bands[PER * g + c, pl.ds((33 - 2 * d) * WIN, 2 * WIN), :]
+                high = bands[PER * g + c, pl.ds((32 - 2 * d) * WIN, 2 * WIN), :]
+                total += jnp.dot(
+                    left, jnp.concatenate([low, high], axis=1), preferred_element_type=F32
+                )
+            for a in range(16):
+                first = ROWS * (4 + a // 4) + 4 * c + a % 4
+                put(work, WORK, first, 16, 4 * ROWS, total[16 * a : 16 * a + 16])
+        for j in range(0, N, 8):
+            block = take(work, WORK, (4 + j) * ROWS, 8 * ROWS).astype(BF16)
+            send_y[g, pl.ds(j, 8)] = block.reshape(8, ROWS, B)
+        recv_y[g, me] = send_y[g, me]
+        send(send_y.at[g], recv_y.at[g], sy.at[g], ry.at[g])
+
+    squares = jnp.zeros((8, B), F32)
+    for g in range(GROUPS):
+        waits(send_y.at[g], recv_y.at[g], sy.at[g], ry.at[g]).wait_recv()
+        for j in range(N):
+            at = pl.ds(j * 16 + g * ROWS, ROWS)
+            gain = skip_t[at, :]
+            gated = send_x[g, j].astype(F32)
+            mixed = take(og_t, T, j * 16 + g * ROWS, ROWS) * (
+                recv_y[g, j].astype(F32) + jnp.concatenate([gain, gain], axis=1) * gated
             )
-        for a in range(16):
-            first = 16 * (a // 4) + 4 * c + a % 4
-            put(stage, SIZE, first, 16, 64, total[16 * a : 16 * a + 16])
-    for j in range(0, N, 8):
-        send_y[pl.ds(j, 8)] = take(stage, SIZE, j * 16, 128).astype(BF16).reshape(8, 16, B)
-    recv_y[me] = send_y[me]
-    send(send_y, recv_y, sy, ry)
-    waits(send_y, recv_y, sy, ry).wait_recv()
-
-    squares = jnp.zeros((8, B), F32)
-    for j in range(0, N, 2):
-        at = pl.ds(j * 16, 32)
-        gain = skip_t[at, :]
-        conv = recv_y[pl.ds(j, 2)].reshape(32, B).astype(F32)
-        gated = send_x[pl.ds(j, 2)].reshape(32, B).astype(F32)
-        mixed = take(og_t, T, j * 16, 32) * (conv + jnp.concatenate([gain, gain], axis=1) * gated)
-        put(stage, SIZE, j * 16, 32, 1, mixed)
-        squares += jnp.sum((mixed * mixed).reshape(4, 8, B), axis=0)
+            put(stage, T, j * 16 + g * ROWS, ROWS, 1, mixed)
+            squares += jnp.sum((mixed * mixed).reshape(ROWS // 8, 8, B), axis=0)
     part[0:4, :] = squares[0:4] + squares[4:8]
     part[4:8, :] = jnp.zeros((4, B), F32)
     copies = []
@@ -186,19 +198,23 @@
         )
         copy.start()
         copies.append(copy)
+    for q in range(4):
+        turned[pl.ds(q * B, B), :] = take(stage, T, q, CH, 4).T
+    waits(send_t, recv_t, st, rt).wait_send()
+    for g in range(GROUPS):
+        waits(send_x.at[g], recv_x.at[g], sx.at[g], rx.at[g]).wait_send()
+        waits(send_y.at[g], recv_y.at[g], sy.at[g], ry.at[g]).wait_send()
     power = part[0:4, :]
     for copy in copies:
         copy.wait_recv()
     power = power + recv_p[0][0:4] + recv_p[1][0:4] + recv_p[2][0:4]
     scale = 1.0 / jnp.sqrt(power / C + 1e-05)
     for q in range(4):
-        mixed = take(stage, SIZE, q, CH, 4) * scale[q : q + 1]
-        out[pl.ds(q * B, B), :] = mixed.T.astype(BF16)
+        column = jnp.broadcast_to(scale[q : q + 1], (128, B)).T
+        column = jnp.concatenate([column, column], axis=1)
+        out[pl.ds(q * B, B), :] = (turned[pl.ds(q * B, B), :] * column).astype(BF16)
     for copy in copies:
         copy.wait_send()
-    waits(send_t, recv_t, st, rt).wait_send()
-    waits(send_x, recv_x, sx, rx).wait_send()
-    waits(send_y, recv_y, sy, ry).wait_send()
 
 
 def local(gate_in, value_in, out_gate, filter_taps, skip_gain):
@@ -215,24 +231,27 @@
             pltpu.VMEM((T, CH), BF16),
             pltpu.VMEM((TAPS, CH), BF16),
             pltpu.VMEM((1, CH), F32),
-            pltpu.VMEM((N, 16, B), BF16),
+            pltpu.VMEM((GROUPS, N, ROWS, B), BF16),
             pltpu.VMEM((N, 1, B), F32),
-            pltpu.VMEM((N, 16, B), BF16),
+            pltpu.VMEM((GROUPS, N, ROWS, B), BF16),
             pltpu.VMEM((N, 1, B), F32),
-            pltpu.VMEM((2 * SIZE, 128), F32),
+            pltpu.VMEM((2 * T, 128), F32),
+            pltpu.VMEM((2 * WORK, 128), F32),
+            pltpu.VMEM((T, CH), F32),
             pltpu.VMEM((2 * T, 128), F32),
             pltpu.VMEM((T, 128), F32),
             pltpu.VMEM((OWN, 40, WIN), F32),
-            pltpu.VMEM((OWN, 512, B), BF16),
+            pltpu.VMEM((PER, 512, B), BF16),
             pltpu.VMEM((OWN, BANDS * WIN, WIN), BF16),
-            pltpu.VMEM((N, 16, B), BF16),
-            pltpu.VMEM((N, 16, B), BF16),
+            pltpu.VMEM((GROUPS, N, ROWS, B), BF16),
+            pltpu.VMEM((GROUPS, N, ROWS, B), BF16),
             pltpu.VMEM((8, B), F32),
             pltpu.VMEM((3, 8, B), F32),
-            dma((5,)), dma, dma, dma, dma, dma, dma, dma((3,)), dma((3,)),
+            dma((5,)), dma((GROUPS,)), dma((GROUPS,)), dma, dma, dma((GROUPS,)), dma((GROUPS,)),
+            dma((3,)), dma((3,)),
         ],
         compiler_params=pltpu.CompilerParams(
-            collective_id=0, has_side_effects=True, vmem_limit_bytes=48 * 2**20
+            collective_id=0, has_side_effects=True, vmem_limit_bytes=67043328
         ),
     )(gate_in, value_in, out_gate, filter_taps, skip_gain.reshape(1, CH))
 

time: 61 us -> 52.3 us (0.86)
  Pallas kernels: 55.4 us -> 50.3 us
  local copies, waits for them, and re-layouts: 5.35 us -> 1.87 us
    pallas_call x1, Pallas kernels: 55.4 us -> 50.3 us  [local(): pl.pallas_call(kernel, out_shape=jax.ShapeDtypeStruct((T, CH), BF16), in_...]
    unnamed x11 -> x1, local copies, waits for them, and re-layouts: 5.35 us -> 1.87 us
where the time goes in v3:
time: 52.3 us; the launch traced here: 52.2 us
  Pallas kernels  50.3 us (96%)
  local copies, waits for them, and re-layouts  1.87 us (4%)
    pallas_call x1, Pallas kernels, local(): pl.pallas_call(kernel, out_shape=jax.ShapeDtypeStruct((T, CH), BF16), in_...  50.3 us
    unnamed x1, local copies, waits for them, and re-layouts  1.87 us

profile of v3, /device:TPU:1, one launch (start us, length us, event | category | flops | bytes accessed | tf_op | source)
XLA Modules:
  0.0 52.2 jit_solution(12035143927379123688)
XLA Ops:
  0.0 50.3 %shard_map.55 = bf16[1024,256]{1,0:T(8,128)(2,1)} custom-call(bf16[1024,256]{1,0:T(8,128)(2,1)} %gate_h.1, bf16[1024,256]{1,0:T(8,128)(2,1)} %value_h.1, bf16[1024,256]{1,0:T(8,128)(2,1)} %out_gate_h.1, bf16[64,256]{1,0:T(8,128)(2,1)} %taps_h.1, f32[1,256]{1,0:T(1,128)} %bitcast.1), custom_call_target="tpu_custom_call" | custom-call | tf_op jit(solution)/shard_map/pallas_call | solution.py:223
  50.3 1.9 %copy.7 = bf16[1024,256]{1,0:T(8,128)(2,1)} copy(bf16[1024,256]{1,0:T(8,128)(2,1)} %shard_map.55) | data formatting | bytes 1048576

commit v4 on v3

v4 whole, which is shorter than its diff:
```python
import jax
import jax.numpy as jnp
from jax import lax
from jax.experimental import pallas as pl
from jax.experimental.pallas import tpu as pltpu
from jax.sharding import PartitionSpec as P

MESH = pl.DeviceIdType.MESH
F32 = jnp.float32
BF16 = jnp.bfloat16

C = 1024
B = 256
N = 64
T = 1024
CH = 256
TAPS = 64
WIN = 128
NWIN = 4096 // WIN
BANDS = 2 * 17 + 1
PER = 2
PAIRS = CH // PER
ROWS = 4 * PER
WORK = (N + 4) * ROWS
OWN = PAIRS // N


def place(me):
    return me // 32, me // 4 % 8, me % 4


ALONG = (4, 3, 5, 2, 6, 1, 7, 0)


def put(ref, size, first, count, stride, value):
    for h in range(2):
        ref[pl.ds(h * size + first, count, stride=stride), :] = value[:, 128 * h : 128 * h + 128]


def take(ref, size, first, count, stride=1):
    halves = [ref[pl.ds(h * size + first, count, stride=stride), :] for h in range(2)]
    return jnp.concatenate(halves, axis=1)


def kernel(
    gate_h, value_h, out_gate_h, taps_h, skip_h, out,
    gate, value, out_gate, taps, skip,
    send_x, send_t, recv_x, recv_t, stage, work, turned, og_t, skip_t, win, planes, bands, send_y, recv_y,
    part, recv_p, loaded, sx, rx, st, rt, sy, ry, sp, rp,
):
    me = lax.axis_index("seq")
    mp = lax.axis_index("mp")
    barrier = pltpu.get_barrier_semaphore()

    x, z, y = place(me)
    along = [(z + dz) % 8 * 4 for dz in ALONG]

    def others(visit):
        def column(r, last):
            dx, dy = (r + 1) % 8 // 4, (r + 1) % 4
            base = (x + dx) % 2 * 32 + (y + dy) % 4
            for plane in along[: 8 - last]:
                visit(base + plane)

        def each(r, carry):
            column(r, 0)
            return carry

        lax.fori_loop(0, 7, each, 0)
        column(7, 1)

    others(
        lambda to: pl.semaphore_signal(
            barrier, inc=1, device_id={"seq": to}, device_id_type=MESH
        )
    )
    for k in range(1, 4):
        pl.semaphore_signal(barrier, inc=1, device_id={"mp": (mp + k) % 4}, device_id_type=MESH)

    pairs = ((taps_h, taps), (gate_h, gate), (value_h, value), (out_gate_h, out_gate), (skip_h, skip))
    loads = [pltpu.make_async_copy(a, b, loaded.at[i]) for i, (a, b) in enumerate(pairs)]
    for load in loads:
        load.start()

    loads[0].wait()
    wide = jnp.concatenate([taps[...].astype(F32), jnp.zeros((128 - TAPS, CH), F32)], axis=0)
    stage[0:CH, :] = wide.T
    first, second = (stage[pl.ds(c, PAIRS, stride=PER), :] for c in range(PER))
    both = first + pltpu.roll(second, 64, 1)
    for j in range(PAIRS):
        send_t[j] = both[j : j + 1]

    loads[1].wait()
    loads[2].wait()
    for q in range(4):
        at = pl.ds(q * B, B)
        gated = (gate[at, :].astype(F32) * value[at, :].astype(F32)).astype(BF16)
        put(stage, T, q, CH, 4, gated.astype(F32).T)
    for j in range(0, N, 8):
        block = take(stage, T, j * 16, 128).astype(BF16)
        send_x[pl.ds(2 * j, 16)] = block.reshape(16, ROWS, B)
    pl.semaphore_wait(barrier, N - 1 + 3)

    def send(src, dst, ssem, rsem, to):
        pltpu.make_async_remote_copy(
            src, dst, ssem, rsem, device_id={"seq": to}, device_id_type=MESH
        ).start()

    def forth_taps(to):
        send(send_t.at[pl.ds(OWN * to, OWN)], recv_t.at[pl.ds(OWN * me, OWN)], st, rt, to)

    def forth(g):
        others(
            lambda to: send(
                send_x.at[OWN * to + g], recv_x.at[g, me], sx.at[g], rx.at[g], to
            )
        )

    def back(g):
        others(
            lambda to: send(
                send_y.at[g, to], recv_y.at[OWN * me + g], sy.at[g], ry.at[g], to
            )
        )

    def of_slabs(ref, n, ssem, rsem):
        return pltpu.make_async_remote_copy(
            ref.at[pl.ds(0, n)], ref.at[pl.ds(0, n)], ssem, rsem,
            device_id={"seq": (me + 1) % N}, device_id_type=MESH,
        )

    others(forth_taps)
    for g in range(OWN):
        forth(g)
    for g in range(OWN):
        recv_t[OWN * me + g] = send_t[OWN * me + g]
        recv_x[g, me] = send_x[OWN * me + g]

    loads[3].wait()
    loads[4].wait()
    for q in range(4):
        put(og_t, T, q, CH, 4, out_gate[pl.ds(q * B, B), :].astype(F32).T)
        skip_t[pl.ds(q, CH, stride=4), :] = jnp.broadcast_to(skip[...], (128, CH)).T

    lane = lax.broadcasted_iota(jnp.int32, (1, WIN), 1)
    win[...] = jnp.zeros_like(win)
    of_slabs(recv_t, OWN * (N - 1), st, rt).wait_recv()
    for g in range(OWN):
        for j in range(NWIN):
            even, odd = recv_t[2 * OWN * j + g], recv_t[OWN * (2 * j + 1) + g]
            win[2 * g, pl.ds(j + 1, 1), :] = jnp.where(lane < 64, even, pltpu.roll(odd, 64, 1))
            win[2 * g + 1, pl.ds(j + 1, 1), :] = jnp.where(lane < 64, pltpu.roll(even, 64, 1), odd)
    after = lax.broadcasted_iota(jnp.int32, (WIN, WIN), 1) >= lax.broadcasted_iota(
        jnp.int32, (WIN, WIN), 0
    )

    def banded(c, carry):
        before = jnp.zeros((WIN, WIN), F32)
        bands[c, pl.ds((BANDS - 1) * WIN, WIN), :] = before.astype(BF16)
        for v in range(NWIN + 1):
            row = jnp.broadcast_to(win[c, v + 1 : v + 2, :], (WIN, WIN))
            rolled = pltpu.roll(row, 0, 1, stride=1, stride_axis=0)
            at = pl.ds((BANDS - 2 - v) * WIN, WIN)
            bands[c, at, :] = jnp.where(after, rolled, before).astype(BF16)
            before = rolled
        bands[c, pl.ds(0, WIN), :] = jnp.zeros((WIN, WIN), BF16)
        return carry

    lax.fori_loop(0, PER * OWN, banded, 0)

    put(work, WORK, 0, 4 * ROWS, 1, jnp.zeros((4 * ROWS, B), F32))

    def convolve(g):
        of_slabs(recv_x.at[g], N - 1, sx.at[g], rx.at[g]).wait_recv()
        for j in range(0, N, 8):
            block = recv_x[g, pl.ds(j, 8)].reshape(8 * ROWS, B).astype(F32)
            put(work, WORK, (4 + j) * ROWS, 8 * ROWS, 1, block)
        for c in range(PER):
            for a in range(16):
                first = ROWS * (a // 4) + 4 * c + a % 4
                for late in range(2):
                    rows = take(work, WORK, first + 4 * ROWS * late, 16, 4 * ROWS)
                    planes[c, pl.ds(256 * late + 16 * a, 16), :] = rows.astype(BF16)
        for c in range(PER):
            total = jnp.zeros((256, B), F32)
            for d in range(17):
                left = planes[c, pl.ds((16 - d) * 16, 256), :]
                low = bands[PER * g + c, pl.ds((33 - 2 * d) * WIN, 2 * WIN), :]
                high = bands[PER * g + c, pl.ds((32 - 2 * d) * WIN, 2 * WIN), :]
                total += jnp.dot(
                    left, jnp.concatenate([low, high], axis=1), preferred_element_type=F32
                )
            for a in range(16):
                first = ROWS * (4 + a // 4) + 4 * c + a % 4
                put(work, WORK, first, 16, 4 * ROWS, total[16 * a : 16 * a + 16])
        for j in range(0, N, 8):
            block = take(work, WORK, (4 + j) * ROWS, 8 * ROWS).astype(BF16)
            send_y[g, pl.ds(j, 8)] = block.reshape(8, ROWS, B)
        recv_y[OWN * me + g] = send_y[g, me]
        back(g)

    for g in range(OWN):
        convolve(g)

    for g in range(OWN):
        of_slabs(recv_y, N - 1, sy.at[g], ry.at[g]).wait_recv()
    squares = jnp.zeros((8, B), F32)
    for j in range(PAIRS):
        at = pl.ds(j * ROWS, ROWS)
        gain = skip_t[at, :]
        mixed = take(og_t, T, j * ROWS, ROWS) * (
            recv_y[j].astype(F32)
            + jnp.concatenate([gain, gain], axis=1) * send_x[j].astype(F32)
        )
        put(stage, T, j * ROWS, ROWS, 1, mixed)
        squares += mixed * mixed
    part[0:4, :] = squares[0:4] + squares[4:8]
    part[4:8, :] = jnp.zeros((4, B), F32)
    copies = []
    for k in range(1, 4):
        copy = pltpu.make_async_remote_copy(
            part, recv_p.at[k - 1], sp.at[k - 1], rp.at[k - 1],
            device_id={"mp": (mp + k) % 4}, device_id_type=MESH,
        )
        copy.start()
        copies.append(copy)
    for q in range(4):
        turned[pl.ds(q * B, B), :] = take(stage, T, q, CH, 4).T
    of_slabs(send_t, OWN * (N - 1), st, rt).wait_send()
    for g in range(OWN):
        of_slabs(send_x, N - 1, sx.at[g], rx.at[g]).wait_send()
        of_slabs(send_y.at[g], N - 1, sy.at[g], ry.at[g]).wait_send()
    power = part[0:4, :]
    for copy in copies:
        copy.wait_recv()
    power = power + recv_p[0][0:4] + recv_p[1][0:4] + recv_p[2][0:4]
    scale = 1.0 / jnp.sqrt(power / C + 1e-05)
    for q in range(4):
        column = jnp.broadcast_to(scale[q : q + 1], (128, B)).T
        column = jnp.concatenate([column, column], axis=1)
        out[pl.ds(q * B, B), :] = (turned[pl.ds(q * B, B), :] * column).astype(BF16)
    for copy in copies:
        copy.wait_send()


def local(gate_in, value_in, out_gate, filter_taps, skip_gain):
    arrays = (gate_in, value_in, out_gate, filter_taps, skip_gain.reshape(1, CH))
    vmem = pl.BlockSpec(memory_space=pltpu.VMEM)
    dma = pltpu.SemaphoreType.DMA
    return pl.pallas_call(
        kernel,
        out_shape=jax.ShapeDtypeStruct((T, CH), BF16),
        in_specs=[pl.BlockSpec(memory_space=pltpu.HBM)] * 5,
        out_specs=vmem,
        scratch_shapes=[
            pltpu.VMEM((T, CH), BF16),
            pltpu.VMEM((T, CH), BF16),
            pltpu.VMEM((T, CH), BF16),
            pltpu.VMEM((TAPS, CH), BF16),
            pltpu.VMEM((1, CH), F32),
            pltpu.VMEM((PAIRS, ROWS, B), BF16),
            pltpu.VMEM((PAIRS, 1, WIN), F32),
            pltpu.VMEM((OWN, N, ROWS, B), BF16),
            pltpu.VMEM((OWN * N, 1, WIN), F32),
            pltpu.VMEM((2 * T, 128), F32),
            pltpu.VMEM((2 * WORK, 128), F32),
            pltpu.VMEM((T, CH), F32),
            pltpu.VMEM((2 * T, 128), F32),
            pltpu.VMEM((T, 128), F32),
            pltpu.VMEM((PER * OWN, 40, WIN), F32),
            pltpu.VMEM((PER, 512, B), BF16),
            pltpu.VMEM((PER * OWN, BANDS * WIN, WIN), BF16),
            pltpu.VMEM((OWN, N, ROWS, B), BF16),
            pltpu.VMEM((PAIRS, ROWS, B), BF16),
            pltpu.VMEM((8, B), F32),
            pltpu.VMEM((3, 8, B), F32),
            dma((5,)), dma((OWN,)), dma((OWN,)), dma, dma, dma((OWN,)), dma((OWN,)), dma((3,)), dma((3,)),
        ],
        compiler_params=pltpu.CompilerParams(
            collective_id=0, has_side_effects=True, vmem_limit_bytes=40 * 2**20
        ),
    )(*[pltpu.with_memory_space_constraint(a, pltpu.HBM) for a in arrays])


def solution(mesh):
    return jax.shard_map(
        local,
        mesh=mesh,
        in_specs=(P("seq", "mp"), P("seq", "mp"), P("seq", "mp"), P("seq", "mp"), P("mp")),
        out_specs=P("seq", "mp"),
        check_vma=False,
    )
```

time: 52.3 us -> 45.7 us (0.87)
  Pallas kernels: 50.3 us -> 44.8 us
  local copies, waits for them, and re-layouts: 1.87 us -> 0.8 us
    pallas_call x1, Pallas kernels: 50.3 us -> 44.8 us  [local(): pl.pallas_call(kernel, out_shape=jax.ShapeDtypeStruct((T, CH), BF16), in_...]
    unnamed x1, local copies, waits for them, and re-layouts: 1.87 us -> 0.8 us
where the time goes in v4:
time: 45.7 us; the launch traced here: 45.6 us
  Pallas kernels  44.8 us (98%)
  local copies, waits for them, and re-layouts  0.8 us (2%)
    pallas_call x1, Pallas kernels, local(): pl.pallas_call(kernel, out_shape=jax.ShapeDtypeStruct((T, CH), BF16), in_...  44.8 us

profile of v4, /device:TPU:1, one launch (start us, length us, event | category | flops | bytes accessed | tf_op | source)
XLA Modules:
  0.0 45.6 jit_solution(13378114870097639515)
XLA Ops:
  0.0 44.8 %shard_map.55 = bf16[1024,256]{1,0:T(8,128)(2,1)S(1)} custom-call(bf16[1024,256]{1,0:T(8,128)(2,1)} %gate_h.1, bf16[1024,256]{1,0:T(8,128)(2,1)} %value_h.1, bf16[1024,256]{1,0:T(8,128)(2,1)} %out_gate_h.1, bf16[64,256]{1,0:T(8,128)(2,1)} %taps_h.1, f32[1,256]{1,0:T(1,128)} %bitcast.1), custom_call_target="tpu_custom_call" | custom-call | tf_op jit(solution)/shard_map/pallas_call | solution.py:250
  44.8 0.8 %copy.7 = bf16[1024,256]{1,0:T(8,128)(2,1)} copy(bf16[1024,256]{1,0:T(8,128)(2,1)S(1)} %shard_map.55) | data formatting | bytes 1048576

commit v5 on v4

--- a/solution.py
+++ b/solution.py
@@ -87,8 +87,8 @@
     stage[0:CH, :] = wide.T
     first, second = (stage[pl.ds(c, PAIRS, stride=PER), :] for c in range(PER))
     both = first + pltpu.roll(second, 64, 1)
-    for j in range(PAIRS):
-        send_t[j] = both[j : j + 1]
+    for j in range(N):
+        send_t[j] = both[OWN * j : OWN * j + OWN].astype(BF16)
 
     loads[1].wait()
     loads[2].wait()
@@ -107,7 +107,7 @@
         ).start()
 
     def forth_taps(to):
-        send(send_t.at[pl.ds(OWN * to, OWN)], recv_t.at[pl.ds(OWN * me, OWN)], st, rt, to)
+        send(send_t.at[to], recv_t.at[me], st, rt, to)
 
     def forth(g):
         others(
@@ -117,11 +117,28 @@
         )
 
     def back(g):
-        others(
-            lambda to: send(
-                send_y.at[g, to], recv_y.at[OWN * me + g], sy.at[g], ry.at[g], to
-            )
-        )
+        for half in range(2):
+            half_planes = [(z + k) % 4 * 4 + 16 * half for k in range(4)]
+
+            def go(to):
+                send(send_y.at[g, to], recv_y.at[OWN * me + g], sy.at[g], ry.at[g], to)
+
+            def column(r, first, half_planes=half_planes, go=go):
+                dx, dy = (r + 1) % 8 // 4, (r + 1) % 4
+                base = (x + dx) % 2 * 32 + (y + dy) % 4
+                for plane in half_planes[first:]:
+                    go(base + plane)
+
+            def each(r, carry, column=column):
+                column(r, 0)
+                return carry
+
+            lax.fori_loop(0, 7, each, 0)
+            column(7, 1)
+
+            @pl.when(z // 4 != half)
+            def _(go=go, plane=half_planes[0]):
+                go(x * 32 + y + plane)
 
     def of_slabs(ref, n, ssem, rsem):
         return pltpu.make_async_remote_copy(
@@ -132,8 +149,8 @@
     others(forth_taps)
     for g in range(OWN):
         forth(g)
-    for g in range(OWN):
-        recv_t[OWN * me + g] = send_t[OWN * me + g]
+    recv_t[me] = send_t[me]
+    for g in range(OWN):
         recv_x[g, me] = send_x[OWN * me + g]
 
     loads[3].wait()
@@ -142,14 +159,16 @@
         put(og_t, T, q, CH, 4, out_gate[pl.ds(q * B, B), :].astype(F32).T)
         skip_t[pl.ds(q, CH, stride=4), :] = jnp.broadcast_to(skip[...], (128, CH)).T
 
-    lane = lax.broadcasted_iota(jnp.int32, (1, WIN), 1)
+    lane = lax.broadcasted_iota(jnp.int32, (OWN, WIN), 1)
     win[...] = jnp.zeros_like(win)
-    of_slabs(recv_t, OWN * (N - 1), st, rt).wait_recv()
-    for g in range(OWN):
-        for j in range(NWIN):
-            even, odd = recv_t[2 * OWN * j + g], recv_t[OWN * (2 * j + 1) + g]
-            win[2 * g, pl.ds(j + 1, 1), :] = jnp.where(lane < 64, even, pltpu.roll(odd, 64, 1))
-            win[2 * g + 1, pl.ds(j + 1, 1), :] = jnp.where(lane < 64, pltpu.roll(even, 64, 1), odd)
+    of_slabs(recv_t, N - 1, st, rt).wait_recv()
+    for j in range(NWIN):
+        even, odd = recv_t[2 * j].astype(F32), recv_t[2 * j + 1].astype(F32)
+        one = jnp.where(lane < 64, even, pltpu.roll(odd, 64, 1))
+        two = jnp.where(lane < 64, pltpu.roll(even, 64, 1), odd)
+        for g in range(OWN):
+            win[2 * g, pl.ds(j + 1, 1), :] = one[g : g + 1]
+            win[2 * g + 1, pl.ds(j + 1, 1), :] = two[g : g + 1]
     after = lax.broadcasted_iota(jnp.int32, (WIN, WIN), 1) >= lax.broadcasted_iota(
         jnp.int32, (WIN, WIN), 0
     )
@@ -226,7 +245,7 @@
         copies.append(copy)
     for q in range(4):
         turned[pl.ds(q * B, B), :] = take(stage, T, q, CH, 4).T
-    of_slabs(send_t, OWN * (N - 1), st, rt).wait_send()
+    of_slabs(send_t, N - 1, st, rt).wait_send()
     for g in range(OWN):
         of_slabs(send_x, N - 1, sx.at[g], rx.at[g]).wait_send()
         of_slabs(send_y.at[g], N - 1, sy.at[g], ry.at[g]).wait_send()
@@ -259,9 +278,9 @@
             pltpu.VMEM((TAPS, CH), BF16),
             pltpu.VMEM((1, CH), F32),
             pltpu.VMEM((PAIRS, ROWS, B), BF16),
-            pltpu.VMEM((PAIRS, 1, WIN), F32),
+            pltpu.VMEM((N, OWN, WIN), BF16),
             pltpu.VMEM((OWN, N, ROWS, B), BF16),
-            pltpu.VMEM((OWN * N, 1, WIN), F32),
+            pltpu.VMEM((N, OWN, WIN), BF16),
             pltpu.VMEM((2 * T, 128), F32),
             pltpu.VMEM((2 * WORK, 128), F32),
             pltpu.VMEM((T, CH), F32),

time: 45.7 us -> 44.4 us (0.972)
  Pallas kernels: 44.8 us -> 43.5 us
    pallas_call x1, Pallas kernels: 44.8 us -> 43.5 us  [local(): pl.pallas_call(kernel, out_shape=jax.ShapeDtypeStruct((T, CH), BF16), in_...]
where the time goes in v5:
time: 44.4 us; the launch traced here: 44.3 us
  Pallas kernels  43.5 us (98%)
  local copies, waits for them, and re-layouts  0.8 us (2%)
    pallas_call x1, Pallas kernels, local(): pl.pallas_call(kernel, out_shape=jax.ShapeDtypeStruct((T, CH), BF16), in_...  43.5 us

profile of v5, /device:TPU:1, one launch (start us, length us, event | category | flops | bytes accessed | tf_op | source)
XLA Modules:
  0.0 44.3 jit_solution(16697498416337277517)
XLA Ops:
  0.0 43.5 %shard_map.55 = bf16[1024,256]{1,0:T(8,128)(2,1)S(1)} custom-call(bf16[1024,256]{1,0:T(8,128)(2,1)} %gate_h.1, bf16[1024,256]{1,0:T(8,128)(2,1)} %value_h.1, bf16[1024,256]{1,0:T(8,128)(2,1)} %out_gate_h.1, bf16[64,256]{1,0:T(8,128)(2,1)} %taps_h.1, f32[1,256]{1,0:T(1,128)} %bitcast.1), custom_call_target="tpu_custom_call" | custom-call | tf_op jit(solution)/shard_map/pallas_call | solution.py:269
  43.5 0.8 %copy.7 = bf16[1024,256]{1,0:T(8,128)(2,1)} copy(bf16[1024,256]{1,0:T(8,128)(2,1)S(1)} %shard_map.55) | data formatting | bytes 1048576

commit v6 on v5

--- a/solution.py
+++ b/solution.py
@@ -18,11 +18,9 @@
 WIN = 128
 NWIN = 4096 // WIN
 BANDS = 2 * 17 + 1
-PER = 2
-PAIRS = CH // PER
-ROWS = 4 * PER
+ROWS = 4
 WORK = (N + 4) * ROWS
-OWN = PAIRS // N
+OWN = CH // N
 
 
 def place(me):
@@ -85,10 +83,10 @@
     loads[0].wait()
     wide = jnp.concatenate([taps[...].astype(F32), jnp.zeros((128 - TAPS, CH), F32)], axis=0)
     stage[0:CH, :] = wide.T
-    first, second = (stage[pl.ds(c, PAIRS, stride=PER), :] for c in range(PER))
+    first, second = (stage[pl.ds(c, CH // 2, stride=2), :] for c in range(2))
     both = first + pltpu.roll(second, 64, 1)
     for j in range(N):
-        send_t[j] = both[OWN * j : OWN * j + OWN].astype(BF16)
+        send_t[j] = both[2 * j : 2 * j + 2].astype(BF16)
 
     loads[1].wait()
     loads[2].wait()
@@ -98,7 +96,7 @@
         put(stage, T, q, CH, 4, gated.astype(F32).T)
     for j in range(0, N, 8):
         block = take(stage, T, j * 16, 128).astype(BF16)
-        send_x[pl.ds(2 * j, 16)] = block.reshape(16, ROWS, B)
+        send_x[pl.ds(OWN * j, 8 * OWN)] = block.reshape(8 * OWN, ROWS, B)
     pl.semaphore_wait(barrier, N - 1 + 3)
 
     def send(src, dst, ssem, rsem, to):
@@ -108,6 +106,27 @@
 
     def forth_taps(to):
         send(send_t.at[to], recv_t.at[me], st, rt, to)
+
+    def by_halves(visit, order):
+        for half in order:
+            half_planes = [(z + k) % 4 * 4 + 16 * half for k in range(4)]
+
+            def column(r, first, half_planes=half_planes):
+                dx, dy = (r + 1) % 8 // 4, (r + 1) % 4
+                base = (x + dx) % 2 * 32 + (y + dy) % 4
+                for plane in half_planes[first:]:
+                    visit(base + plane)
+
+            def each(r, carry, column=column):
+                column(r, 0)
+                return carry
+
+            lax.fori_loop(0, 7, each, 0)
+            column(7, 1)
+
+            @pl.when(z // 4 != half)
+            def _(plane=half_planes[0]):
+                visit(x * 32 + y + plane)
 
     def forth(g):
         others(
@@ -116,29 +135,13 @@
             )
         )
 
-    def back(g):
-        for half in range(2):
-            half_planes = [(z + k) % 4 * 4 + 16 * half for k in range(4)]
-
-            def go(to):
-                send(send_y.at[g, to], recv_y.at[OWN * me + g], sy.at[g], ry.at[g], to)
-
-            def column(r, first, half_planes=half_planes, go=go):
-                dx, dy = (r + 1) % 8 // 4, (r + 1) % 4
-                base = (x + dx) % 2 * 32 + (y + dy) % 4
-                for plane in half_planes[first:]:
-                    go(base + plane)
-
-            def each(r, carry, column=column):
-                column(r, 0)
-                return carry
-
-            lax.fori_loop(0, 7, each, 0)
-            column(7, 1)
-
-            @pl.when(z // 4 != half)
-            def _(go=go, plane=half_planes[0]):
-                go(x * 32 + y + plane)
+    def back(g, halves):
+        by_halves(
+            lambda to: send(
+                send_y.at[g, to], recv_y.at[OWN * me + g], sy.at[g], ry.at[g], to
+            ),
+            halves,
+        )
 
     def of_slabs(ref, n, ssem, rsem):
         return pltpu.make_async_remote_copy(
@@ -159,14 +162,14 @@
         put(og_t, T, q, CH, 4, out_gate[pl.ds(q * B, B), :].astype(F32).T)
         skip_t[pl.ds(q, CH, stride=4), :] = jnp.broadcast_to(skip[...], (128, CH)).T
 
-    lane = lax.broadcasted_iota(jnp.int32, (OWN, WIN), 1)
+    lane = lax.broadcasted_iota(jnp.int32, (2, WIN), 1)
     win[...] = jnp.zeros_like(win)
     of_slabs(recv_t, N - 1, st, rt).wait_recv()
     for j in range(NWIN):
         even, odd = recv_t[2 * j].astype(F32), recv_t[2 * j + 1].astype(F32)
         one = jnp.where(lane < 64, even, pltpu.roll(odd, 64, 1))
         two = jnp.where(lane < 64, pltpu.roll(even, 64, 1), odd)
-        for g in range(OWN):
+        for g in range(2):
             win[2 * g, pl.ds(j + 1, 1), :] = one[g : g + 1]
             win[2 * g + 1, pl.ds(j + 1, 1), :] = two[g : g + 1]
     after = lax.broadcasted_iota(jnp.int32, (WIN, WIN), 1) >= lax.broadcasted_iota(
@@ -185,7 +188,7 @@
         bands[c, pl.ds(0, WIN), :] = jnp.zeros((WIN, WIN), BF16)
         return carry
 
-    lax.fori_loop(0, PER * OWN, banded, 0)
+    lax.fori_loop(0, OWN, banded, 0)
 
     put(work, WORK, 0, 4 * ROWS, 1, jnp.zeros((4 * ROWS, B), F32))
 
@@ -194,47 +197,45 @@
         for j in range(0, N, 8):
             block = recv_x[g, pl.ds(j, 8)].reshape(8 * ROWS, B).astype(F32)
             put(work, WORK, (4 + j) * ROWS, 8 * ROWS, 1, block)
-        for c in range(PER):
-            for a in range(16):
-                first = ROWS * (a // 4) + 4 * c + a % 4
-                for late in range(2):
-                    rows = take(work, WORK, first + 4 * ROWS * late, 16, 4 * ROWS)
-                    planes[c, pl.ds(256 * late + 16 * a, 16), :] = rows.astype(BF16)
-        for c in range(PER):
-            total = jnp.zeros((256, B), F32)
-            for d in range(17):
-                left = planes[c, pl.ds((16 - d) * 16, 256), :]
-                low = bands[PER * g + c, pl.ds((33 - 2 * d) * WIN, 2 * WIN), :]
-                high = bands[PER * g + c, pl.ds((32 - 2 * d) * WIN, 2 * WIN), :]
-                total += jnp.dot(
-                    left, jnp.concatenate([low, high], axis=1), preferred_element_type=F32
-                )
-            for a in range(16):
-                first = ROWS * (4 + a // 4) + 4 * c + a % 4
-                put(work, WORK, first, 16, 4 * ROWS, total[16 * a : 16 * a + 16])
+        for a in range(16):
+            first = ROWS * (a // 4) + a % 4
+            for late in range(2):
+                rows = take(work, WORK, first + 4 * ROWS * late, 16, 4 * ROWS)
+                planes[pl.ds(256 * late + 16 * a, 16), :] = rows.astype(BF16)
+        total = jnp.zeros((256, B), F32)
+        for d in range(17):
+            left = planes[pl.ds((16 - d) * 16, 256), :]
+            low = bands[g, pl.ds((33 - 2 * d) * WIN, 2 * WIN), :]
+            high = bands[g, pl.ds((32 - 2 * d) * WIN, 2 * WIN), :]
+            total += jnp.dot(left, jnp.concatenate([low, high], axis=1), preferred_element_type=F32)
+        for a in range(16):
+            first = ROWS * (4 + a // 4) + a % 4
+            put(work, WORK, first, 16, 4 * ROWS, total[16 * a : 16 * a + 16])
         for j in range(0, N, 8):
             block = take(work, WORK, (4 + j) * ROWS, 8 * ROWS).astype(BF16)
             send_y[g, pl.ds(j, 8)] = block.reshape(8, ROWS, B)
         recv_y[OWN * me + g] = send_y[g, me]
-        back(g)
+        back(g, (0, 1) if g < OWN - 2 else (0,))
 
     for g in range(OWN):
         convolve(g)
-
+    for g in range(OWN - 2, OWN):
+        back(g, (1,))
+
+    squares = jnp.zeros((8, B), F32)
     for g in range(OWN):
         of_slabs(recv_y, N - 1, sy.at[g], ry.at[g]).wait_recv()
-    squares = jnp.zeros((8, B), F32)
-    for j in range(PAIRS):
-        at = pl.ds(j * ROWS, ROWS)
+    for j in range(0, CH, 2):
+        at = pl.ds(j * ROWS, 2 * ROWS)
         gain = skip_t[at, :]
-        mixed = take(og_t, T, j * ROWS, ROWS) * (
-            recv_y[j].astype(F32)
-            + jnp.concatenate([gain, gain], axis=1) * send_x[j].astype(F32)
-        )
-        put(stage, T, j * ROWS, ROWS, 1, mixed)
+        conv = recv_y[pl.ds(j, 2)].reshape(2 * ROWS, B).astype(F32)
+        gated = send_x[pl.ds(j, 2)].reshape(2 * ROWS, B).astype(F32)
+        mixed = take(og_t, T, j * ROWS, 2 * ROWS) * (
+            conv + jnp.concatenate([gain, gain], axis=1) * gated
+        )
+        put(stage, T, j * ROWS, 2 * ROWS, 1, mixed)
         squares += mixed * mixed
-    part[0:4, :] = squares[0:4] + squares[4:8]
-    part[4:8, :] = jnp.zeros((4, B), F32)
+    part[...] = squares[0:4] + squares[4:8]
     copies = []
     for k in range(1, 4):
         copy = pltpu.make_async_remote_copy(
@@ -249,10 +250,10 @@
     for g in range(OWN):
         of_slabs(send_x, N - 1, sx.at[g], rx.at[g]).wait_send()
         of_slabs(send_y.at[g], N - 1, sy.at[g], ry.at[g]).wait_send()
-    power = part[0:4, :]
+    power = part[...]
     for copy in copies:
         copy.wait_recv()
-    power = power + recv_p[0][0:4] + recv_p[1][0:4] + recv_p[2][0:4]
+    power = power + recv_p[0] + recv_p[1] + recv_p[2]
     scale = 1.0 / jnp.sqrt(power / C + 1e-05)
     for q in range(4):
         column = jnp.broadcast_to(scale[q : q + 1], (128, B)).T
@@ -277,22 +278,22 @@
             pltpu.VMEM((T, CH), BF16),
             pltpu.VMEM((TAPS, CH), BF16),
             pltpu.VMEM((1, CH), F32),
-            pltpu.VMEM((PAIRS, ROWS, B), BF16),
-            pltpu.VMEM((N, OWN, WIN), BF16),
+            pltpu.VMEM((CH, ROWS, B), BF16),
+            pltpu.VMEM((N, 2, WIN), BF16),
             pltpu.VMEM((OWN, N, ROWS, B), BF16),
-            pltpu.VMEM((N, OWN, WIN), BF16),
+            pltpu.VMEM((N, 2, WIN), BF16),
             pltpu.VMEM((2 * T, 128), F32),
             pltpu.VMEM((2 * WORK, 128), F32),
             pltpu.VMEM((T, CH), F32),
             pltpu.VMEM((2 * T, 128), F32),
             pltpu.VMEM((T, 128), F32),
-            pltpu.VMEM((PER * OWN, 40, WIN), F32),
-            pltpu.VMEM((PER, 512, B), BF16),
-            pltpu.VMEM((PER * OWN, BANDS * WIN, WIN), BF16),
+            pltpu.VMEM((OWN, 40, WIN), F32),
+            pltpu.VMEM((512, B), BF16),
+            pltpu.VMEM((OWN, BANDS * WIN, WIN), BF16),
             pltpu.VMEM((OWN, N, ROWS, B), BF16),
-            pltpu.VMEM((PAIRS, ROWS, B), BF16),
-            pltpu.VMEM((8, B), F32),
-            pltpu.VMEM((3, 8, B), F32),
+            pltpu.VMEM((CH, ROWS, B), BF16),
+            pltpu.VMEM((4, B), F32),
+            pltpu.VMEM((3, 4, B), F32),
             dma((5,)), dma((OWN,)), dma((OWN,)), dma, dma, dma((OWN,)), dma((OWN,)), dma((3,)), dma((3,)),
         ],
         compiler_params=pltpu.CompilerParams(

time: 44.4 us -> 43.9 us (0.989)
  Pallas kernels: 43.5 us -> 43 us
where the time goes in v6:
time: 43.9 us; the launch traced here: 43.8 us
  Pallas kernels  43 us (98%)
  local copies, waits for them, and re-layouts  0.8 us (2%)
    pallas_call x1, Pallas kernels, local(): pl.pallas_call(kernel, out_shape=jax.ShapeDtypeStruct((T, CH), BF16), in_...  43 us

profile of v6, /device:TPU:1, one launch (start us, length us, event | category | flops | bytes accessed | tf_op | source)
XLA Modules:
  0.0 43.8 jit_solution(17719222406015028216)
XLA Ops:
  0.0 43.0 %shard_map.55 = bf16[1024,256]{1,0:T(8,128)(2,1)S(1)} custom-call(bf16[1024,256]{1,0:T(8,128)(2,1)} %gate_h.1, bf16[1024,256]{1,0:T(8,128)(2,1)} %value_h.1, bf16[1024,256]{1,0:T(8,128)(2,1)} %out_gate_h.1, bf16[64,256]{1,0:T(8,128)(2,1)} %taps_h.1, f32[1,256]{1,0:T(1,128)} %bitcast.1), custom_call_target="tpu_custom_call" | custom-call | tf_op jit(solution)/shard_map/pallas_call | solution.py:270
  43.0 0.8 %copy.7 = bf16[1024,256]{1,0:T(8,128)(2,1)} copy(bf16[1024,256]{1,0:T(8,128)(2,1)S(1)} %shard_map.55) | data formatting | bytes 1048576

commit v7 on v6

--- a/solution.py
+++ b/solution.py
@@ -223,18 +223,19 @@
         back(g, (1,))
 
     squares = jnp.zeros((8, B), F32)
-    for g in range(OWN):
-        of_slabs(recv_y, N - 1, sy.at[g], ry.at[g]).wait_recv()
-    for j in range(0, CH, 2):
-        at = pl.ds(j * ROWS, 2 * ROWS)
-        gain = skip_t[at, :]
-        conv = recv_y[pl.ds(j, 2)].reshape(2 * ROWS, B).astype(F32)
-        gated = send_x[pl.ds(j, 2)].reshape(2 * ROWS, B).astype(F32)
-        mixed = take(og_t, T, j * ROWS, 2 * ROWS) * (
-            conv + jnp.concatenate([gain, gain], axis=1) * gated
-        )
-        put(stage, T, j * ROWS, 2 * ROWS, 1, mixed)
-        squares += mixed * mixed
+    for g in range(0, OWN, 2):
+        for h in (g, g + 1):
+            of_slabs(recv_y, N - 1, sy.at[h], ry.at[h]).wait_recv()
+        for j in range(g, CH, OWN):
+            at = pl.ds(j * ROWS, 2 * ROWS)
+            gain = skip_t[at, :]
+            conv = recv_y[pl.ds(j, 2)].reshape(2 * ROWS, B).astype(F32)
+            gated = send_x[pl.ds(j, 2)].reshape(2 * ROWS, B).astype(F32)
+            mixed = take(og_t, T, j * ROWS, 2 * ROWS) * (
+                conv + jnp.concatenate([gain, gain], axis=1) * gated
+            )
+            put(stage, T, j * ROWS, 2 * ROWS, 1, mixed)
+            squares += mixed * mixed
     part[...] = squares[0:4] + squares[4:8]
     copies = []
     for k in range(1, 4):

time: 43.9 us -> 43.8 us (level)
  no operation moved by 1% of the time
where the time goes in v7:
time: 43.8 us; the launch traced here: 43.7 us
  Pallas kernels  42.9 us (98%)
  local copies, waits for them, and re-layouts  0.8 us (2%)
    pallas_call x1, Pallas kernels, local(): pl.pallas_call(kernel, out_shape=jax.ShapeDtypeStruct((T, CH), BF16), in_...  42.9 us

profile of v7, /device:TPU:1, one launch (start us, length us, event | category | flops | bytes accessed | tf_op | source)
XLA Modules:
  0.0 43.7 jit_solution(15046931299263869005)
XLA Ops:
  0.0 42.9 %shard_map.55 = bf16[1024,256]{1,0:T(8,128)(2,1)S(1)} custom-call(bf16[1024,256]{1,0:T(8,128)(2,1)} %gate_h.1, bf16[1024,256]{1,0:T(8,128)(2,1)} %value_h.1, bf16[1024,256]{1,0:T(8,128)(2,1)} %out_gate_h.1, bf16[64,256]{1,0:T(8,128)(2,1)} %taps_h.1, f32[1,256]{1,0:T(1,128)} %bitcast.1), custom_call_target="tpu_custom_call" | custom-call | tf_op jit(solution)/shard_map/pallas_call | solution.py:271
  42.9 0.8 %copy.7 = bf16[1024,256]{1,0:T(8,128)(2,1)} copy(bf16[1024,256]{1,0:T(8,128)(2,1)S(1)} %shard_map.55) | data formatting | bytes 1048576
